TPU v7x, 32 devices: a whole 2x2x4 slice. The times are simulated.
32 devices in a mesh: row: 4 (over z), col: 4 (over y, core), rep: 2 (over x).
Axes of the slice: x: 2, y: 2, z: 4, core: 2. Of those that a mesh axis runs over, the one named last changes fastest.
Arguments:
- upstream: float32 [16384, 16384], P('row', ('col', 'rep')), may hold values from -0.046875 to 0.046875
- input_panel: float32 [16384, 1024], P('row', ('col', 'rep')), may hold values from -6 to 6
Outputs:
- panel_grad: float32 [16384, 1024], P('row', ('col', 'rep'))
All inputs are finite; a program needn't handle non-finite values.
Results may differ from a plain program's by a relative error of at most 0.000071.
Values sent between devices are 32-bit elements; how exact they have to be, the bound alone decides.
A program may use at most 192 MiB of HBM per device.

v0:
```python
import jax
import jax.numpy as jnp
from jax import lax
from jax.sharding import PartitionSpec as P


def from_root(x, axis, root):
    mine = lax.axis_index(axis) == root
    return lax.psum(jnp.where(mine, x, jnp.zeros_like(x)), axis)


def row_total(buffer):
    return lax.psum_scatter(buffer, "row", scatter_dimension=0, tiled=True)


def per_device(upstream, input_panel):
    precise = lax.Precision.HIGHEST
    row_count, col_count = upstream.shape
    row_index = lax.axis_index("row")
    col_index = lax.axis_index(("col", "rep"))
    rows_global = row_index * row_count + lax.broadcasted_iota(jnp.int32, (row_count, col_count), 0)
    cols_global = col_index * col_count + lax.broadcasted_iota(jnp.int32, (row_count, col_count), 1)
    lower_tile = jnp.where(cols_global <= rows_global, upstream, jnp.float32(0.0))
    row_band = lax.all_gather(input_panel, ("col", "rep"), axis=1, tiled=True)
    upper_part = lax.dot_general(
        lower_tile,
        row_band,
        (((0,), (0,)), ((), ())),
        precision=precise,
        preferred_element_type=jnp.float32,
    )
    source_row = col_index * col_count // row_count
    offset = col_index * col_count - source_row * row_count
    column_rows = from_root(
        lax.dynamic_slice_in_dim(row_band, offset, col_count, 0), "row", source_row
    )
    buffer = lax.all_to_all(upper_part, ("col", "rep"), split_axis=1, concat_axis=0, tiled=True)
    lower_total = lax.psum_scatter(
        lax.dot_general(
            column_rows,
            lower_tile,
            (((0,), (1,)), ((), ())),
            precision=precise,
            preferred_element_type=jnp.float32,
        ),
        ("col", "rep"),
        scatter_dimension=0,
        tiled=True,
    )
    return row_total(buffer) + jnp.transpose(lower_total)


def solution(mesh):
    placed = (P("row", ("col", "rep")), P("row", ("col", "rep")))
    return jax.shard_map(
        per_device, mesh=mesh, in_specs=placed, out_specs=P("row", ("col", "rep")), check_vma=False
    )
```

profile of v0, /device:TPU:0, one launch (start us, length us, event | category | flops | bytes accessed | tf_op | source)
XLA Modules:
  0.0 751.1 jit_solution(11321924936020843688)
XLA Ops:
  6.5 0.0 all-gather.2.cloned.1.call-start
  6.5 0.7 all-gather.2.cloned.1.call-update
  7.3 0.0 all-reduce.2.cloned.1.call-start
  7.4 23.6 %compare_select_fusion.7 = f32[4096,2048]{1,0:T(8,128)} fusion(f32[4096,2048]{1,0:T(8,128)} %param.2, s32[2048]{0:T(1024)S(1)} %iota_add_fusion.1, s32[4096]{0:T(1024)S(1)} %iota_add_fusion), kind=kLoop, calls=%fused_computation.clone.1.clone.1 | loop fusion | flops 16777216 | bytes 67133440 | tf_op jit(solution)/shard_map/dot_general | solution.py:25
  30.9 74.0 %all-gather.2.cloned.1.call-done = f32[4096,1024]{1,0:T(8,128)} async-done(((f32[4096,128]{1,0:T(8,128)}), f32[4096,1024]{1,0:T(8,128)}) %all-gather.2.cloned.1.call-update) | async-done | bytes 16777232 | tf_op jit(solution)/shard_map/all_gather | solution.py:24
  105.0 8.5 %dynamic-slice_select_fusion = f32[2048,1024]{1,0:T(8,128)} fusion(f32[4096,1024]{1,0:T(8,128)} %all-gather.2.cloned.1.call-done, s32[]{:T(128)S(6)} %select_n.23, pred[]{:T(512)S(6)} %eq.3), kind=kLoop, calls=%fused_computation.9 | loop fusion | flops 2097152 | bytes 16777220 | tf_op jit(solution)/shard_map/jit(_where)/select_n | solution.py:9
  113.5 0.0 all-reduce.2.cloned.1.call-update
  113.5 0.0 reduce-scatter.3.cloned.1.call-start
  113.6 124.2 %fusion.1 = f32[2048,1024]{0,1:T(8,128)S(1)} fusion(f32[4096,1024]{1,0:T(8,128)} %all-gather.2.cloned.1.call-done, f32[4096,2048]{1,0:T(8,128)} %compare_select_fusion.7), kind=kOutput, calls=%fused_computation.2 | convolution fusion | flops 103079215104 | bytes 58720256 | tf_op jit(solution)/shard_map/dot_general | solution.py:25
  237.7 96.0 %all_to_all.19 = f32[2048,8,128]{0,2,1:T(8,128)S(1)} all-to-all(f32[2048,8,128]{0,2,1:T(8,128)S(1)} %bitcast.13), channel_id=1, replica_groups=mesh['row'=4,'col'=4,'rep'=2] {'col','rep'}, dimensions={1} | all-to-all | bytes 16777216 | tf_op jit(solution)/shard_map/all_to_all | solution.py:37
  333.7 3.8 copy.5
  337.5 0.0 reduce-scatter.3.cloned.1.call-update
  337.5 0.0 reduce-scatter.5.cloned.1.call-start
  337.6 66.9 %all-reduce.2.cloned.1.call-done = f32[2048,1024]{1,0:T(8,128)} async-done(((f32[2048,1024]{1,0:T(8,128)}), f32[2048,1024]{1,0:T(8,128)}) %all-reduce.2.cloned.1.call-update) | async-done | bytes 8388624 | tf_op jit(solution)/shard_map/psum | solution.py:9
  404.5 220.5 %fusion = f32[1024,4096]{1,0:T(8,128)} fusion(f32[2048,1024]{1,0:T(8,128)} %all-reduce.2.cloned.1.call-done, f32[4096,2048]{1,0:T(8,128)} %param.2, s32[2048]{0:T(1024)S(1)} %iota_add_fusion.1, s32[4096]{0:T(1024)S(1)} %iota_add_fusion), kind=kOutput, calls=%fused_computation.1 | convolution fusion | flops 103095992320 | bytes 58744832 | tf_op jit(solution)/shard_map/dot_general | solution.py:39
  625.0 0.0 reduce-scatter.5.cloned.1.call-update
  625.0 0.0 reduce-scatter.3.cloned.1.call-done
  625.1 115.3 %reduce-scatter.5.cloned.1.call-done = f32[128,4096]{1,0:T(8,128)} async-done(((f32[1024,4096]{1,0:T(8,128)}), f32[128,4096]{1,0:T(8,128)}) %reduce-scatter.5.cloned.1.call-update) | async-done | bytes 2097168 | tf_op jit(solution)/shard_map/reduce_scatter | solution.py:38
  740.3 2.4 bitcast_add_fusion
  742.8 1.8 copy.4
  (2 shorter events, 0.0 us)
Async XLA Ops:
  6.5 98.5 %all-gather.2.cloned.1.call-start = ((), (), s32[]{:S(2)}) async-start(), calls=%async_computation.3 | async-start | bytes 18874368 | tf_op jit(solution)/shard_map/all_gather | solution.py:24
  7.3 397.2 %all-reduce.2.cloned.1.call-start = ((), (), s32[]{:S(2)}) async-start(), calls=%async_computation.5 | async-start | bytes 16777216 | tf_op jit(solution)/shard_map/psum | solution.py:9
  113.5 511.6 %reduce-scatter.3.cloned.1.call-start = ((), (), s32[]{:S(2)}) async-start(), calls=%async_computation.4 | async-start | bytes 10485760 | tf_op jit(solution)/shard_map/reduce_scatter | solution.py:13
  337.5 402.8 %reduce-scatter.5.cloned.1.call-start = ((), (), s32[]{:S(2)}) async-start(), calls=%async_computation.6 | async-start | bytes 18874368 | tf_op jit(solution)/shard_map/reduce_scatter | solution.py:38
Sparse Core Ops, SparseCore 0:
  9.2 95.7 all-gather.1
  113.6 290.8 all-reduce.1
  406.9 143.5 reduce-scatter.2
  625.2 115.1 reduce-scatter.4
where the time goes:
time: 751 us
  matrix products  345 us (46%)
  waiting for transfers between devices  257 us (34%)
  blocking collectives  96 us (13%)
  other arithmetic  34.5 us (5%)
  between operations  13.2 us (2%)
    dot_general x1, matrix products, per_device(): lax.dot_general(column_rows, lower_tile, (((0,), (1,)), ((), ())), precis...  221 us
    dot_general x1, matrix products, per_device(): lax.dot_general(lower_tile, row_band, (((0,), (0,)), ((), ())), precision...  124 us
    reduce_scatter x1, waiting for transfers between devices, per_device(): lax.psum_scatter(lax.dot_general(column_rows, lower_tile, (((0,), (1,)),...  115 us
    all_to_all x1, blocking collectives, per_device(): lax.all_to_all(upper_part, ('col', 'rep'), split_axis=1, concat_axis=0, t...  96 us
    all_gather x1, waiting for transfers between devices, per_device(): row_band = lax.all_gather(input_panel, ('col', 'rep'), axis=1, tiled=True)  74 us
    psum x1, waiting for transfers between devices, from_root(): return lax.psum(jnp.where(mine, x, jnp.zeros_like(x)), axis)  66.9 us
    dot_general x1, other arithmetic, per_device(): lax.dot_general(lower_tile, row_band, (((0,), (0,)), ((), ())), precision...  23.6 us
  transfers between devices with their start and end apart: 4, of which 3 were waited for; matrix products, arithmetic and copies ran while one was open for 50% of the time, Pallas kernels for 0%

commit v1 on v0

--- a/solution.py
+++ b/solution.py
@@ -34,7 +34,9 @@
     column_rows = from_root(
         lax.dynamic_slice_in_dim(row_band, offset, col_count, 0), "row", source_row
     )
-    buffer = lax.all_to_all(upper_part, ("col", "rep"), split_axis=1, concat_axis=0, tiled=True)
+    shards = jnp.split(upper_part, lax.axis_size(("col", "rep")), axis=1)
+    incoming = lax.all_to_all(jnp.stack(shards), ("col", "rep"), 0, 0)
+    buffer = jnp.concatenate(incoming, axis=0)
     lower_total = lax.psum_scatter(
         lax.dot_general(
             column_rows,

time: 751 us -> 881 us (1.17)
  waiting for transfers between devices: 257 us -> 366 us
  local copies, waits for them, and re-layouts: 5.61 us -> 24.5 us
    psum x1, waiting for transfers between devices: 66.9 us -> 176 us  [from_root(): return lax.psum(jnp.where(mine, x, jnp.zeros_like(x)), axis)]
    unnamed x0 -> x9, local copies, waits for them, and re-layouts: none -> 11.1 us
    reshape x0 -> x1, local copies, waits for them, and re-layouts: none -> 8.99 us  [per_device(): buffer = jnp.concatenate(incoming, axis=0)]
  transfers between devices with their start and end apart: 4 -> 4, of which waited for: 3 -> 3; matrix products, arithmetic and copies ran while one was open for 50% -> 30% of each run, Pallas kernels for 0% -> 0%
where the time goes in v1:
time: 881 us
  waiting for transfers between devices  366 us (42%)
  matrix products  343 us (39%)
  blocking collectives  99.1 us (11%)
  other arithmetic  34.5 us (4%)
  local copies, waits for them, and re-layouts  24.5 us (3%)
  between operations  13.2 us (1%)
    dot_general x1, matrix products, per_device(): lax.dot_general(column_rows, lower_tile, (((0,), (1,)), ((), ())), precis...  221 us
    psum x1, waiting for transfers between devices, from_root(): return lax.psum(jnp.where(mine, x, jnp.zeros_like(x)), axis)  176 us
    dot_general x1, matrix products, per_device(): lax.dot_general(lower_tile, row_band, (((0,), (0,)), ((), ())), precision...  123 us
    reduce_scatter x1, waiting for transfers between devices, per_device(): lax.psum_scatter(lax.dot_general(column_rows, lower_tile, (((0,), (1,)),...  115 us
    all_to_all x1, blocking collectives, per_device(): incoming = lax.all_to_all(jnp.stack(shards), ('col', 'rep'), 0, 0)  99.1 us
    all_gather x1, waiting for transfers between devices, per_device(): row_band = lax.all_gather(input_panel, ('col', 'rep'), axis=1, tiled=True)  74 us
    dot_general x1, other arithmetic, per_device(): lax.dot_general(lower_tile, row_band, (((0,), (0,)), ((), ())), precision...  23.6 us
  transfers between devices with their start and end apart: 4, of which 3 were waited for; matrix products, arithmetic and copies ran while one was open for 30% of the time, Pallas kernels for 0%

profile of v1, /device:TPU:0, one launch (start us, length us, event | category | flops | bytes accessed | tf_op | source)
XLA Modules:
  0.0 880.6 jit_solution(3866380555979826320)
XLA Ops:
  6.5 0.7 all-gather.2.cloned.1.call-update
  7.3 0.0 all-reduce.2.cloned.1.call-start
  7.4 23.6 %compare_select_fusion.7 = f32[4096,2048]{1,0:T(8,128)} fusion(f32[4096,2048]{1,0:T(8,128)} %param.2, s32[2048]{0:T(1024)S(1)} %iota_add_fusion.1, s32[4096]{0:T(1024)S(1)} %iota_add_fusion), kind=kLoop, calls=%fused_computation.clone.1.clone.1 | loop fusion | flops 16777216 | bytes 67133440 | tf_op jit(solution)/shard_map/dot_general | solution.py:25
  30.9 74.0 %all-gather.2.cloned.1.call-done = f32[4096,1024]{1,0:T(8,128)} async-done(((f32[4096,128]{1,0:T(8,128)}), f32[4096,1024]{1,0:T(8,128)}) %all-gather.2.cloned.1.call-update) | async-done | bytes 16777232 | tf_op jit(solution)/shard_map/all_gather | solution.py:24
  105.0 122.8 %fusion.1 = f32[2048,1024]{1,0:T(8,128)S(1)} fusion(f32[4096,1024]{1,0:T(8,128)} %all-gather.2.cloned.1.call-done, f32[4096,2048]{1,0:T(8,128)} %compare_select_fusion.7), kind=kOutput, calls=%fused_computation.2 | convolution fusion | flops 103079215104 | bytes 58720256 | tf_op jit(solution)/shard_map/dot_general | solution.py:25
  227.9 1.3 fusion.15
  229.2 1.7 fusion.14
  230.8 1.3 fusion.13
  232.1 1.1 fusion.12
  233.2 1.2 fusion.11
  234.4 8.5 dynamic-slice_select_fusion
  242.9 0.0 reduce-scatter.3.cloned.1.call-start
  243.0 2.3 fusion.10
  245.2 2.3 fusion.9
  247.5 2.6 fusion.8
  250.1 99.1 %all_to_all.5 = f32[8,2048,128]{2,1,0:T(8,128)} all-to-all(f32[8,2048,128]{2,1,0:T(8,128)} %fusion.8), channel_id=1, replica_groups=mesh['row'=4,'col'=4,'rep'=2] {'col','rep'}, dimensions={0} | all-to-all | bytes 16777216 | tf_op jit(solution)/shard_map/all_to_all | solution.py:38
  349.2 9.0 %copy.3 = f32[16384,128]{0,1:T(8,128)} copy(f32[16384,128]{1,0:T(8,128)} %bitcast.40) | data formatting | bytes 16777216 | tf_op jit(solution)/shard_map/reshape | solution.py:39
  358.2 0.0 reduce-scatter.5.cloned.1.call-start
  358.3 175.6 %all-reduce.2.cloned.1.call-done = f32[2048,1024]{1,0:T(8,128)} async-done(((f32[2048,1024]{1,0:T(8,128)}), f32[2048,1024]{1,0:T(8,128)}) %all-reduce.2.cloned.1.call-update) | async-done | bytes 8388624 | tf_op jit(solution)/shard_map/psum | solution.py:9
  533.9 220.5 %fusion = f32[1024,4096]{1,0:T(8,128)} fusion(f32[2048,1024]{1,0:T(8,128)} %all-reduce.2.cloned.1.call-done, f32[4096,2048]{1,0:T(8,128)} %param.2, s32[2048]{0:T(1024)S(1)} %iota_add_fusion.1, s32[4096]{0:T(1024)S(1)} %iota_add_fusion), kind=kOutput, calls=%fused_computation.1 | convolution fusion | flops 103095992320 | bytes 58744832 | tf_op jit(solution)/shard_map/dot_general | solution.py:41
  754.5 0.0 reduce-scatter.3.cloned.1.call-done
  754.5 115.3 %reduce-scatter.5.cloned.1.call-done = f32[128,4096]{1,0:T(8,128)} async-done(((f32[1024,4096]{1,0:T(8,128)}), f32[128,4096]{1,0:T(8,128)}) %reduce-scatter.5.cloned.1.call-update) | async-done | bytes 2097168 | tf_op jit(solution)/shard_map/reduce_scatter | solution.py:40
  869.8 2.4 bitcast_add_fusion
  872.2 1.8 copy.4
  (8 shorter events, 0.1 us)
Async XLA Ops:
  6.5 98.5 %all-gather.2.cloned.1.call-start = ((), (), s32[]{:S(2)}) async-start(), calls=%async_computation.3 | async-start | bytes 18874368 | tf_op jit(solution)/shard_map/all_gather | solution.py:24
  7.3 526.7 %all-reduce.2.cloned.1.call-start = ((), (), s32[]{:S(2)}) async-start(), calls=%async_computation.5 | async-start | bytes 16777216 | tf_op jit(solution)/shard_map/psum | solution.py:9
  227.8 5.4 copy-start
  242.9 511.6 %reduce-scatter.3.cloned.1.call-start = ((), (), s32[]{:S(2)}) async-start(), calls=%async_computation.4 | async-start | bytes 10485760 | tf_op jit(solution)/shard_map/reduce_scatter | solution.py:13
  358.2 511.6 %reduce-scatter.5.cloned.1.call-start = ((), (), s32[]{:S(2)}) async-start(), calls=%async_computation.6 | async-start | bytes 18874368 | tf_op jit(solution)/shard_map/reduce_scatter | solution.py:40
Sparse Core Ops, SparseCore 0:
  9.2 95.7 all-gather.1
  243.1 290.8 all-reduce.1
  536.3 143.5 reduce-scatter.2
  754.6 115.1 reduce-scatter.4
